TPU v7x, 256 devices: a whole 4x4x8 slice. The times are simulated.
256 devices in a mesh: dp: 8 (over z_lo, core), cent: 32 (over y, z_hi, x).
Axes of the slice: x: 4, y: 4, z: 8 (z_hi: 2, z_lo: 4; z = z_hi * 4 + z_lo), core: 2. Of those that a mesh axis runs over, the one named last changes fastest.
Arguments:
- embeddings: bfloat16 [32768, 768], P(('dp', 'cent')), may hold values from -20 to 20
- fine_centroids: float32 [16384, 768], P('cent'), may hold values from -8 to 8
- parents: int32 [16384], P('cent'), may hold values from 0 to 2047
- coarse_centroids: float32 [2048, 768], P('cent'), may hold values from -6 to 6
Outputs:
- new_fine: float32 [16384, 768], P('cent')
- new_coarse: float32 [2048, 768], P('cent')
All inputs are finite; a program needn't handle non-finite values.
Results may differ from a plain program's by a relative error of at most 0.004.
Values may be sent and summed in bfloat16 or wider, within the bound.
No kernel may reach another device: no remote copies, remote signals or barrier semaphores. Data moves between devices by JAX's collectives and lax.ppermute only.
A program may use at most 64 MiB of HBM per device.

v0:
```python
import math
import jax
import jax.numpy as jnp
from jax import lax
from jax.sharding import PartitionSpec as P

KC = 2048
sharpness = 0.1
coarse_prior = 16.0


def copy_for_each(array, axis):
    devices = lax.axis_size(axis)
    return lax.all_to_all(
        jnp.broadcast_to(array[None], (devices, *array.shape)), axis, 0, 0, tiled=True
    )


def collected_together(array, axis):
    leaves = jax.tree.leaves(array)
    turns = sorted(range(len(leaves)), key=lambda k: -leaves[k].size)
    width = (1, *leaves[turns[0]].shape)[-1]
    lines = [
        jnp.pad(leaves[k].reshape(-1), (0, -leaves[k].size % width)).reshape(-1, width)
        for k in turns
    ]
    both, at, found = (copy_for_each(jnp.concatenate(lines), axis), 0, {})
    for k, line in zip(turns, lines):
        piece = both[:, at : at + len(line)].reshape(len(both), -1)
        found[k] = piece[:, : leaves[k].size].reshape(-1, *leaves[k].shape)
        at += len(line)
    numbers = iter(range(len(leaves)))
    return jax.tree.map(lambda _: found[next(numbers)], array)


def joined_by_halves(pieces, combine):
    while len(jax.tree.leaves(pieces)[0]) > 1:
        pieces = jax.vmap(combine)(
            *(jax.tree.map(lambda part: part[side::2], pieces) for side in (0, 1))
        )
    return jax.tree.map(lambda part: part[0], pieces)


def joined_all(array, axis, combine):
    pieces = collected_together(array, axis)
    return joined_by_halves(pieces, combine)


def cut_along(array, dim, devices):
    dims = array.shape
    tiles = array.reshape(*dims[:dim], devices, dims[dim] // devices, *dims[dim + 1 :])
    return jnp.moveaxis(tiles, dim, 0)


def summed_on_arrival(array, axis, dim):
    tiles = cut_along(array, dim, lax.axis_size(axis))
    arrived = lax.all_to_all(tiles, axis, split_axis=0, concat_axis=0, tiled=True)
    return arrived.sum(axis=0)


def side_by_side(arrays, axis, dim, along):
    widths = [math.prod(a.shape[along:]) for a in arrays]
    both = jnp.concatenate(
        [a.reshape(*a.shape[:along], w) for a, w in zip(arrays, widths)], axis=along
    )
    whole = summed_on_arrival(both, axis, dim)
    tiles = jnp.split(whole, [sum(widths[:k]) for k in range(1, len(widths))], axis=along)
    return tuple((b.reshape(*whole.shape[:along], *a.shape[along:]) for a, b in zip(arrays, tiles)))


def in_order(tiles, dim):
    dims = list(tiles.shape[1:])
    dims[dim] *= tiles.shape[0]
    return jnp.moveaxis(tiles, 0, dim).reshape(dims)


def gather_directly(array, axis, dim):
    tiles = copy_for_each(array, axis)
    return in_order(tiles, dim)


def block_logits(one_block, narrow_centroids, half_norm):
    scores = lax.dot_general(
        one_block, narrow_centroids, (((1,), (1,)), ((), ())), preferred_element_type=jnp.float32
    )
    return sharpness * (scores - half_norm[None, :])


def merge_stats(former, latter):
    highest = jnp.maximum(former[0], latter[0])
    combined = former[1] * jnp.exp(former[0] - highest) + latter[1] * jnp.exp(latter[0] - highest)
    return (highest, combined)


def coarse_terms(parent_ids, pooled, mass_rows):
    summed = jax.ops.segment_sum(pooled, parent_ids, num_segments=KC)
    weighted = jax.ops.segment_sum(mass_rows, parent_ids, num_segments=KC)
    return (summed, weighted)


def local(embeddings, fine_centroids, parents, coarse_centroids):
    gathered = lax.all_gather(embeddings, "cent", axis=0, tiled=True)
    row_count = gathered.shape[0]
    feat_width = gathered.shape[1]
    block_rows = math.gcd(row_count, 512)
    row_blocks = gathered.reshape(row_count // block_rows, block_rows, feat_width)
    narrow_centroids = fine_centroids.astype(jnp.bfloat16)
    half_norm = 0.5 * jnp.sum(fine_centroids * fine_centroids, axis=1)
    no_carry = jnp.zeros((), jnp.float32)

    def stats_step(carried, one_block):
        logits = block_logits(one_block, narrow_centroids, half_norm)
        highest = jnp.max(logits, axis=1)
        return (carried, (highest, jnp.sum(jnp.exp(logits - highest[:, None]), axis=1)))

    _, (local_peak, local_mass) = lax.scan(stats_step, no_carry, row_blocks)
    row_peak, row_mass = joined_all(
        (local_peak.reshape(-1), local_mass.reshape(-1)), "cent", merge_stats
    )

    def sum_step(carried, items):
        one_block, block_peak, block_mass = items
        logits = block_logits(one_block, narrow_centroids, half_norm)
        soft_weights = jnp.exp(logits - block_peak[:, None]) / block_mass[:, None]
        wide_block = one_block.astype(jnp.float32)
        summed = carried[0] + lax.dot_general(
            soft_weights,
            wide_block,
            (((0,), (0,)), ((), ())),
            precision=lax.Precision.HIGHEST,
            preferred_element_type=jnp.float32,
        )
        counted = carried[1] + jnp.sum(soft_weights, axis=0)
        return ((summed, counted), None)

    local_rows = fine_centroids.shape[0]
    start_state = (
        jnp.zeros(fine_centroids.shape, jnp.float32),
        jnp.zeros((local_rows,), jnp.float32),
    )
    stacked = (row_blocks, row_peak.reshape(-1, block_rows), row_mass.reshape(-1, block_rows))
    (fine_sums, fine_counts), _ = lax.scan(sum_step, start_state, stacked)
    total_sums, total_counts = lax.psum((fine_sums, fine_counts), "dp")
    pooled = fine_centroids + total_sums
    mass_rows = 1.0 + total_counts
    new_fine = pooled / mass_rows[:, None]
    col_width = feat_width // lax.axis_size("dp")
    first_col = lax.axis_index("dp") * col_width
    pooled_cols = lax.dynamic_slice_in_dim(pooled, first_col, col_width, 1)
    coarse_sum, coarse_mass = coarse_terms(parents, pooled_cols, mass_rows)
    owned_sum, owned_mass = side_by_side((coarse_sum, coarse_mass), "cent", 0, 1)
    old_cols = lax.dynamic_slice_in_dim(coarse_centroids, first_col, col_width, 1)
    new_cols = (coarse_prior * old_cols + owned_sum) / (coarse_prior + owned_mass)[:, None]
    new_coarse = gather_directly(new_cols, "dp", 1)
    return (new_fine, new_coarse)


def solution(mesh):
    in_specs = (P(("dp", "cent"), None), P("cent", None), P("cent"), P("cent", None))
    out_specs = (P("cent", None), P("cent", None))
    return jax.shard_map(local, mesh=mesh, in_specs=in_specs, out_specs=out_specs, check_vma=False)
```

profile of v0, /device:TPU:1, one launch (start us, length us, event | category | flops | bytes accessed | tf_op | source)
XLA Modules:
  0.0 385.6 jit_solution(6488801156989215922)
XLA Ops:
  7.2 0.7 all-gather.2.cloned.1.call-update
  7.9 2.2 multiply_reduce_fusion
  10.1 135.7 %all-gather.2.cloned.1.call-done = bf16[4096,768]{1,0:T(8,128)(2,1)} async-done(((bf16[128,768]{1,0:T(8,128)(2,1)}), bf16[4096,768]{1,0:T(8,128)(2,1)}) %all-gather.2.cloned.1.call-update) | async-done | bytes 6291472 | tf_op jit(solution)/shard_map/all_gather | solution.py:102
  145.9 16.8 %while.25 = (s32[]{:T(128)}, f32[8,512]{1,0:T(8,128)S(1)}, f32[8,512]{1,0:T(8,128)S(1)}, bf16[8,512,768]{2,1,0:T(8,128)(2,1)}, bf16[512,768]{1,0:T(8,128)(2,1)S(1)}, /*index=5*/f32[512]{0:T(512)S(1)}, s32[]{:T(128)}, s32[]{:T(128)}) while((s32[]{:T(128)}, f32[8,512]{1,0:T(8,128)S(1)}, f32[8,512]{1,0:T(8,128)S(1)}, ...), condition=%wide.region_4.5_spmd, body=%wide.region_1.4_spmd.sunk | while | flops 403962880 | bytes 3686505 | solution.py:116
  145.9 1.7 fusion.36
  147.6 0.2 exponential_reduce_fusion.2
  147.9 1.8 fusion.36
  150.0 1.8 fusion.36
  151.8 0.2 exponential_reduce_fusion.2
  152.1 1.8 fusion.36
  154.2 1.8 fusion.36
  156.3 1.8 fusion.36
  158.4 1.8 fusion.36
  160.5 1.8 fusion.36
  162.7 1.4 broadcast_in_dim.44
  164.2 5.3 %all-to-all-start = ((f32[32,2,4096]{2,1,0:T(2,128)}), f32[32,2,4096]{2,1,0:T(2,128)S(1)}, u32[]{:S(2)}, u32[]{:S(2)}) async-start(f32[32,2,4096]{2,1,0:T(2,128)} %broadcast_in_dim.44), calls=%async_computation | async-start | bytes 2097152 | tf_op jit(solution)/shard_map/all_to_all | solution.py:14
  169.5 18.9 %all-to-all-done = f32[32,2,4096]{2,1,0:T(2,128)S(1)} async-done(((f32[32,2,4096]{2,1,0:T(2,128)}), f32[32,2,4096]{2,1,0:T(2,128)S(1)}, u32[]{:S(2)}, u32[]{:S(2)}) %all-to-all-start) | async-done | bytes 1048608 | tf_op jit(solution)/shard_map/all_to_all | solution.py:14
  188.4 1.2 fusion.25
  189.6 0.6 copy_bitcast_fusion
  192.7 40.9 %while.26 = (s32[]{:T(128)}, f32[512,768]{1,0:T(8,128)S(1)}, f32[512]{0:T(512)S(1)}, bf16[8,512,768]{2,1,0:T(8,128)(2,1)}, bf16[512,768]{1,0:T(8,128)(2,1)S(1)},...) while((s32[]{:T(128)}, f32[512,768]{1,0:T(8,128)S(1)}, ...), condition=%wide.region_7.8_spmd.clone, body=%wide.region_5.7_spmd.clone.sunk | while | flops 2820669952 | bytes 7624836 | solution.py:142
  192.7 1.9 fusion.40
  194.6 3.2 select_add_fusion.4
  197.8 1.9 fusion.40
  199.7 3.2 select_add_fusion.4
  202.9 1.9 fusion.40
  204.8 3.2 select_add_fusion.4
  208.0 1.9 fusion.40
  209.9 3.2 select_add_fusion.4
  213.2 1.9 fusion.40
  215.0 3.2 select_add_fusion.4
  218.3 1.9 fusion.40
  220.2 3.2 select_add_fusion.4
  223.4 1.9 fusion.40
  225.3 3.2 select_add_fusion.4
  228.5 1.9 fusion.40
  230.4 3.2 select_add_fusion.4
  233.6 1.1 copy-done
  234.8 22.7 %psum.15 = f32[512]{0:T(512)S(1)} all-reduce(f32[512]{0:T(512)S(1)} %get-tuple-element.81), channel_id=1, replica_groups=mesh['dp'=8,'cent'=32] {'dp'}, use_global_device_ids=true, to_apply=%region_9.10 | all-reduce | flops 512 | bytes 4096 | tf_op jit(solution)/shard_map/psum | solution.py:143
  257.5 3.4 scatter_custom_fusion.1
  260.9 0.9 concatenate.15
  261.8 56.3 %all-reduce.2.cloned.1.call-done = f32[512,768]{1,0:T(8,128)} async-done(((f32[512,768]{1,0:T(8,128)}), f32[512,768]{1,0:T(8,128)}) %all-reduce.2.cloned.1.call-update) | async-done | bytes 1572880 | tf_op jit(solution)/shard_map/psum | solution.py:143
  318.1 3.3 broadcast_divide_fusion
  321.4 3.1 scatter_custom_fusion
  324.5 0.3 pad_maximum_fusion
  324.9 36.6 %all_to_all.15 = f32[32,64,97]{2,1,0:T(8,128)S(1)} all-to-all(f32[32,64,97]{2,1,0:T(8,128)S(1)} %pad_maximum_fusion), channel_id=1, replica_groups=mesh['dp'=8,'cent'=32] {'cent'}, dimensions={0} | all-to-all | bytes 1589248 | tf_op jit(solution)/shard_map/all_to_all | solution.py:57
  361.8 0.9 fusion.18
  362.8 15.0 %all_to_all.16 = f32[8,64,96]{2,1,0:T(8,128)S(1)} all-to-all(f32[8,64,96]{2,1,0:T(8,128)S(1)} %broadcast_in_dim.48), channel_id=1, replica_groups=mesh['dp'=8,'cent'=32] {'dp'}, dimensions={0} | all-to-all | bytes 393216 | tf_op jit(solution)/shard_map/all_to_all | solution.py:14
  378.0 0.8 reshape.47
  (84 shorter events, 5.2 us)
Async XLA Ops:
  7.2 138.7 %all-gather.2.cloned.1.call-start = ((), (), s32[]{:S(2)}) async-start(), calls=%async_computation.3 | async-start | bytes 6488064 | tf_op jit(solution)/shard_map/all_gather | solution.py:102
  162.6 1.5 copy-start.2
  164.2 24.2 %all-to-all-start = ((f32[32,2,4096]{2,1,0:T(2,128)}), f32[32,2,4096]{2,1,0:T(2,128)S(1)}, u32[]{:S(2)}, u32[]{:S(2)}) async-start(f32[32,2,4096]{2,1,0:T(2,128)} %broadcast_in_dim.44), calls=%async_computation | async-start | bytes 2097152 | tf_op jit(solution)/shard_map/all_to_all | solution.py:14
  169.4 148.7 %all-reduce.2.cloned.1.call-start = ((), (), s32[]{:S(2)}) async-start(), calls=%async_computation.4 | async-start | bytes 3145728 | tf_op jit(solution)/shard_map/psum | solution.py:143
  191.0 1.6 copy-start.3
  233.6 1.1 copy-start
  233.6 84.5 %copy-start.1 = (f32[512,768]{1,0:T(8,128)S(1)}, f32[512,768]{1,0:T(8,128)}, u32[]{:S(2)}) copy-start(f32[512,768]{1,0:T(8,128)} %param.9) | copy-start | bytes 4718596
Sparse Core Ops, SparseCore 0:
  11.4 134.4 all-gather.1
  234.9 83.1 all-reduce.1
where the time goes:
time: 387 us; the launch traced here: 386 us
  waiting for transfers between devices  212 us (55%)
  blocking collectives  74.4 us (19%)
  matrix products  54.4 us (14%)
  other arithmetic  15.7 us (4%)
  between operations  14.4 us (4%)
  local copies, waits for them, and re-layouts  9.1 us (2%)
  starting transfers between devices  5.35 us (1%)
    all_gather x1, waiting for transfers between devices, local(): gathered = lax.all_gather(embeddings, 'cent', axis=0, tiled=True)  136 us
    psum x1, waiting for transfers between devices, local(): total_sums, total_counts = lax.psum((fine_sums, fine_counts), 'dp')  56.3 us
    all_to_all x1, blocking collectives, summed_on_arrival(): lax.all_to_all(tiles, axis, split_axis=0, concat_axis=0, tiled=True)  36.6 us
    dot_general x16, matrix products, block_logits(): lax.dot_general(one_block, narrow_centroids, (((1,), (1,)), ((), ())), pr...  29 us
    dot_general x8, matrix products, sum_step(): lax.dot_general(soft_weights, wide_block, (((0,), (0,)), ((), ())), preci...  25.5 us
    psum x1, blocking collectives, local(): total_sums, total_counts = lax.psum((fine_sums, fine_counts), 'dp')  22.7 us
    all_to_all x1, waiting for transfers between devices, copy_for_each(): lax.all_to_all(jnp.broadcast_to(array[None], (devices, *array.shape)), ax...  18.9 us
    all_to_all x1, blocking collectives, copy_for_each(): lax.all_to_all(jnp.broadcast_to(array[None], (devices, *array.shape)), ax...  15 us
  transfers between devices with their start and end apart: 3, of which 3 were waited for; matrix products, arithmetic and copies ran while one was open for 2% of the time, Pallas kernels for 0%

commit v1 on v0

--- a/solution.py
+++ b/solution.py
@@ -99,7 +99,9 @@
 
 
 def local(embeddings, fine_centroids, parents, coarse_centroids):
-    gathered = lax.all_gather(embeddings, "cent", axis=0, tiled=True)
+    gathered = jnp.concatenate(
+        lax.all_to_all(jnp.stack([embeddings] * lax.axis_size("cent")), "cent", 0, 0), axis=0
+    )
     row_count = gathered.shape[0]
     feat_width = gathered.shape[1]
     block_rows = math.gcd(row_count, 512)

time: 387 us -> 418 us (1.080)
  waiting for transfers between devices: 212 us -> 157 us
  starting transfers between devices: 5.35 us -> 55.5 us
  blocking collectives: 74.4 us -> 108 us
  local copies, waits for them, and re-layouts: 9.1 us -> 13.4 us
    all_gather x1 -> x0, waiting for transfers between devices: 136 us -> none  [local(): gathered = lax.all_gather(embeddings, 'cent', axis=0, tiled=True)]
    all_to_all x0 -> x1, waiting for transfers between devices: none -> 87.9 us  [local(): lax.all_to_all(jnp.stack([embeddings] * lax.axis_size('cent')), 'cent', 0...]
    all_to_all x1, starting transfers between devices: 5.27 us -> 40.8 us  [copy_for_each(): lax.all_to_all(jnp.broadcast_to(array[None], (devices, *array.shape)), ax...]
    psum x1, blocking collectives: 22.7 us -> 56.4 us  [local(): total_sums, total_counts = lax.psum((fine_sums, fine_counts), 'dp')]
    all_to_all x0 -> x1, starting transfers between devices: none -> 14.7 us  [local(): lax.all_to_all(jnp.stack([embeddings] * lax.axis_size('cent')), 'cent', 0...]
    another operation x0 -> x1, local copies, waits for them, and re-layouts: none -> 4.3 us  [local(): jnp.stack([embeddings] * lax.axis_size('cent'))]
  transfers between devices with their start and end apart: 3 -> 3, of which waited for: 3 -> 3; matrix products, arithmetic and copies ran while one was open for 2% -> 1% of each run, Pallas kernels for 0% -> 0%
where the time goes in v1:
time: 418 us; the launch traced here: 417 us
  waiting for transfers between devices  157 us (38%)
  blocking collectives  108 us (26%)
  starting transfers between devices  55.5 us (13%)
  matrix products  54 us (13%)
  between operations  14.4 us (3%)
  other arithmetic  13.8 us (3%)
  local copies, waits for them, and re-layouts  13.4 us (3%)
    all_to_all x1, waiting for transfers between devices, local(): lax.all_to_all(jnp.stack([embeddings] * lax.axis_size('cent')), 'cent', 0...  87.9 us
    psum x1, blocking collectives, local(): total_sums, total_counts = lax.psum((fine_sums, fine_counts), 'dp')  56.4 us
    psum x1, waiting for transfers between devices, local(): total_sums, total_counts = lax.psum((fine_sums, fine_counts), 'dp')  54.1 us
    all_to_all x1, starting transfers between devices, copy_for_each(): lax.all_to_all(jnp.broadcast_to(array[None], (devices, *array.shape)), ax...  40.8 us
    all_to_all x1, blocking collectives, summed_on_arrival(): lax.all_to_all(tiles, axis, split_axis=0, concat_axis=0, tiled=True)  36.6 us
    dot_general x16, matrix products, block_logits(): lax.dot_general(one_block, narrow_centroids, (((1,), (1,)), ((), ())), pr...  29 us
    dot_general x8, matrix products, sum_step(): lax.dot_general(soft_weights, wide_block, (((0,), (0,)), ((), ())), preci...  25 us
    all_to_all x1, blocking collectives, copy_for_each(): lax.all_to_all(jnp.broadcast_to(array[None], (devices, *array.shape)), ax...  15 us
  transfers between devices with their start and end apart: 3, of which 3 were waited for; matrix products, arithmetic and copies ran while one was open for 1% of the time, Pallas kernels for 0%

profile of v1, /device:TPU:1, one launch (start us, length us, event | category | flops | bytes accessed | tf_op | source)
XLA Modules:
  0.0 416.6 jit_solution(7228256148137498698)
XLA Ops:
  7.2 4.3 %stack.2 = bf16[32,128,768]{2,1,0:T(8,128)(2,1)} broadcast(bf16[128,768]{1,0:T(8,128)(2,1)} %param.8), dimensions={1,2} | broadcast | bytes 6488064 | tf_op jit(solution)/shard_map/stack | solution.py:103
  11.5 14.7 %all-to-all-start = ((bf16[32,128,768]{2,1,0:T(8,128)(2,1)}), bf16[32,128,768]{2,1,0:T(8,128)(2,1)}, u32[]{:S(2)}, u32[]{:S(2)}) async-start(bf16[32,128,768]{2,1,0:T(8,128)(2,1)} %stack.2), calls=%async_computation | async-start | bytes 12582912 | tf_op jit(solution)/shard_map/all_to_all | solution.py:103
  26.4 87.9 %all-to-all-done = bf16[32,128,768]{2,1,0:T(8,128)(2,1)} async-done(((bf16[32,128,768]{2,1,0:T(8,128)(2,1)}), bf16[32,128,768]{2,1,0:T(8,128)(2,1)}, u32[]{:S(2)}, u32[]{:S(2)}) %all-to-all-start) | async-done | bytes 6291488 | tf_op jit(solution)/shard_map/all_to_all | solution.py:103
  114.3 16.8 %while.25 = (s32[]{:T(128)}, f32[8,512]{1,0:T(8,128)S(1)}, f32[8,512]{1,0:T(8,128)S(1)}, bf16[8,512,768]{2,1,0:T(8,128)(2,1)}, bf16[512,768]{1,0:T(8,128)(2,1)S(1)}, /*index=5*/f32[512]{0:T(512)S(1)}, s32[]{:T(128)}, s32[]{:T(128)}) while((s32[]{:T(128)}, f32[8,512]{1,0:T(8,128)S(1)}, f32[8,512]{1,0:T(8,128)S(1)}, ...), condition=%wide.region_4.5_spmd, body=%wide.region_1.4_spmd.sunk | while | flops 403962880 | bytes 3687005 | solution.py:118
  114.3 1.8 fusion.36
  116.1 0.2 exponential_reduce_fusion.2
  116.4 1.8 fusion.36
  118.2 0.2 exponential_reduce_fusion.2
  118.5 1.8 fusion.36
  120.6 1.8 fusion.36
  122.7 1.8 fusion.36
  124.8 1.8 fusion.36
  126.9 1.8 fusion.36
  129.0 1.8 fusion.36
  131.2 1.4 broadcast_in_dim.44
  132.7 40.8 %all-to-all-start.1 = ((f32[32,2,4096]{2,1,0:T(2,128)}), f32[32,2,4096]{2,1,0:T(2,128)S(1)}, u32[]{:S(2)}, u32[]{:S(2)}) async-start(f32[32,2,4096]{2,1,0:T(2,128)} %broadcast_in_dim.44), calls=%async_computation.1 | async-start | bytes 2097152 | tf_op jit(solution)/shard_map/all_to_all | solution.py:14
  173.5 14.8 %all-to-all-done.1 = f32[32,2,4096]{2,1,0:T(2,128)S(1)} async-done(((f32[32,2,4096]{2,1,0:T(2,128)}), f32[32,2,4096]{2,1,0:T(2,128)S(1)}, u32[]{:S(2)}, u32[]{:S(2)}) %all-to-all-start.1) | async-done | bytes 1048608 | tf_op jit(solution)/shard_map/all_to_all | solution.py:14
  188.3 1.2 fusion.25
  189.5 0.6 copy_bitcast_fusion
  192.6 40.5 %while.26 = (s32[]{:T(128)}, f32[512,768]{1,0:T(8,128)S(1)}, f32[512]{0:T(512)S(1)}, bf16[8,512,768]{2,1,0:T(8,128)(2,1)}, bf16[512,768]{1,0:T(8,128)(2,1)S(1)},...) while((s32[]{:T(128)}, f32[512,768]{1,0:T(8,128)S(1)}, ...), condition=%wide.region_7.8_spmd.clone, body=%wide.region_5.7_spmd.clone.sunk | while | flops 2820669952 | bytes 7625844 | solution.py:144
  192.6 1.9 fusion.40
  194.5 3.1 select_add_fusion.4
  197.6 1.9 fusion.40
  199.5 3.1 select_add_fusion.4
  202.7 1.9 fusion.40
  204.6 3.1 select_add_fusion.4
  207.8 1.9 fusion.40
  209.7 3.1 select_add_fusion.4
  212.8 1.9 fusion.40
  214.7 3.1 select_add_fusion.4
  217.9 1.9 fusion.40
  219.8 3.1 select_add_fusion.4
  223.0 1.9 fusion.40
  224.8 3.1 select_add_fusion.4
  228.0 1.9 fusion.40
  229.9 3.1 select_add_fusion.4
  233.1 1.1 copy-done
  234.2 56.4 %psum.15 = f32[512]{0:T(512)S(1)} all-reduce(f32[512]{0:T(512)S(1)} %get-tuple-element.81), channel_id=1, replica_groups=mesh['dp'=8,'cent'=32] {'dp'}, use_global_device_ids=true, to_apply=%region_9.10 | all-reduce | flops 512 | bytes 4096 | tf_op jit(solution)/shard_map/psum | solution.py:145
  290.6 3.6 scatter_custom_fusion.1
  294.2 0.9 concatenate.15
  295.1 54.1 %all-reduce.2.cloned.1.call-done = f32[512,768]{1,0:T(8,128)} async-done(((f32[512,768]{1,0:T(8,128)}), f32[512,768]{1,0:T(8,128)}) %all-reduce.2.cloned.1.call-update) | async-done | bytes 1572880 | tf_op jit(solution)/shard_map/psum | solution.py:145
  349.1 3.3 broadcast_divide_fusion
  352.4 3.1 scatter_custom_fusion
  355.6 0.3 pad_maximum_fusion
  355.9 36.6 %all_to_all.20 = f32[32,64,97]{2,1,0:T(8,128)S(1)} all-to-all(f32[32,64,97]{2,1,0:T(8,128)S(1)} %pad_maximum_fusion), channel_id=1, replica_groups=mesh['dp'=8,'cent'=32] {'cent'}, dimensions={0} | all-to-all | bytes 1589248 | tf_op jit(solution)/shard_map/all_to_all | solution.py:57
  392.8 0.9 fusion.18
  393.8 15.0 %all_to_all.21 = f32[8,64,96]{2,1,0:T(8,128)S(1)} all-to-all(f32[8,64,96]{2,1,0:T(8,128)S(1)} %broadcast_in_dim.48), channel_id=1, replica_groups=mesh['dp'=8,'cent'=32] {'dp'}, dimensions={0} | all-to-all | bytes 393216 | tf_op jit(solution)/shard_map/all_to_all | solution.py:14
  409.0 0.8 reshape.45
  (86 shorter events, 5.3 us)
Async XLA Ops:
  11.5 14.8 %copy-start.1 = (f32[512,768]{1,0:T(8,128)S(1)}, f32[512,768]{1,0:T(8,128)}, u32[]{:S(2)}) copy-start(f32[512,768]{1,0:T(8,128)} %param.9) | copy-start | bytes 4718596
  11.5 102.9 %all-to-all-start = ((bf16[32,128,768]{2,1,0:T(8,128)(2,1)}), bf16[32,128,768]{2,1,0:T(8,128)(2,1)}, u32[]{:S(2)}, u32[]{:S(2)}) async-start(bf16[32,128,768]{2,1,0:T(8,128)(2,1)} %stack.2), calls=%async_computation | async-start | bytes 12582912 | tf_op jit(solution)/shard_map/all_to_all | solution.py:103
  131.1 1.5 copy-start.3
  132.7 55.7 %all-to-all-start.1 = ((f32[32,2,4096]{2,1,0:T(2,128)}), f32[32,2,4096]{2,1,0:T(2,128)S(1)}, u32[]{:S(2)}, u32[]{:S(2)}) async-start(f32[32,2,4096]{2,1,0:T(2,128)} %broadcast_in_dim.44), calls=%async_computation.1 | async-start | bytes 2097152 | tf_op jit(solution)/shard_map/all_to_all | solution.py:14
  173.4 175.7 %all-reduce.2.cloned.1.call-start = ((), (), s32[]{:S(2)}) async-start(), calls=%async_computation.4 | async-start | bytes 3145728 | tf_op jit(solution)/shard_map/psum | solution.py:145
  190.9 1.6 copy-start.4
  233.1 1.1 copy-start
  233.1 116.1 %copy-start.2 = (f32[512,768]{1,0:T(8,128)S(1)}, f32[512,768]{1,0:T(8,128)}, u32[]{:S(2)}) copy-start(f32[512,768]{1,0:T(8,128)} %param.9) | copy-start | bytes 4718596
Sparse Core Ops, SparseCore 0:
  234.3 114.7 all-reduce.1
